TPU v7x, 32 devices: a whole 2x2x4 slice. The times are simulated.
32 devices in a mesh: parts: 2 (over y), expert: 4 (over z), tensor: 4 (over x, core).
Axes of the slice: x: 2, y: 2, z: 4, core: 2. Of those that a mesh axis runs over, the one named last changes fastest.
Arguments:
- mamba_input: bfloat16 [128, 4096], P(('parts', 'expert'), 'tensor'), parts along dimension 0, may hold values from -5 to 5
- mamba_gate: bfloat16 [128, 4096], P(('parts', 'expert'), 'tensor'), parts along dimension 0, may hold values from -5 to 5
- conv_state: bfloat16 [128, 3, 4096], P(('parts', 'expert'), None, 'tensor'), parts along dimension 0, may hold values from -5 to 5
- scan_state: float32 [128, 16, 4096], P(('parts', 'expert'), None, 'tensor'), parts along dimension 0, may hold values from -6 to 6
- conv_weight: float32 [4, 4096], P(None, 'tensor'), may hold values from -3 to 3
- conv_bias: float32 [4096], P('tensor'), may hold values from -0.5 to 0.5
- state_proj: bfloat16 [288, 4096], P(None, 'tensor'), may hold values from -0.09375 to 0.09375
- step_proj: bfloat16 [256, 4096], P(None, 'tensor'), may hold values from -0.375 to 0.375
- step_bias: float32 [4096], P('tensor'), may hold values from -4.5 to -1
- decay_log: float32 [16, 4096], P(None, 'tensor'), may hold values from 0 to 2.8
- skip_gain: float32 [4096], P('tensor'), may hold values from 0.5 to 2
- queries: bfloat16 [128, 32, 128], P(('parts', 'expert'), 'tensor'), parts along dimension 0, may hold values from -48 to 48
- new_entry: bfloat16 [128, 8, 256], P(('parts', 'expert'), 'tensor'), parts along dimension 0, may hold values from -4 to 4
- past_entries: bfloat16 [128, 8, 128, 256], P(('parts', 'expert'), 'tensor'), parts along dimension 0, may hold values from -4 to 4
- lengths: int32 [128], P(('parts', 'expert')), parts along dimension 0, may hold values from 2 to 128, as said below
- expert_input: bfloat16 [128, 2048], P(('parts', 'expert'), 'tensor'), parts along dimension 0, may hold values from -5 to 5
- routes: int32 [128, 2], P(('parts', 'expert')), parts along dimension 0, may hold values from 0 to 7, as said below
- slots: int32 [128, 2], P(('parts', 'expert')), parts along dimension 0, may hold values from 0 to 7, as said below
- gates: float32 [128, 2], P(('parts', 'expert')), parts along dimension 0, may hold values from 0.1 to 1
- inner_weights: bfloat16 [8, 2, 8192, 2048], P('expert', None, 'tensor'), may hold values from -0.125 to 0.125
- outer_weights: bfloat16 [8, 8192, 2048], P('expert', 'tensor'), may hold values from -0.09375 to 0.09375
Outputs:
- mamba_out: bfloat16 [128, 4096], P(('parts', 'expert'), 'tensor'), parts along dimension 0
- next_state: float32 [128, 16, 4096], P(('parts', 'expert'), None, 'tensor'), parts along dimension 0
- attention_out: bfloat16 [128, 4096], P(('parts', 'expert'), 'tensor'), parts along dimension 0
- expert_out: bfloat16 [128, 2048], P(('parts', 'expert'), 'tensor'), parts along dimension 0
There are 2 independent parts, one for each index of `parts`. A program takes and returns all parts, laid end to end along the dimension named above; an argument that names none is the same for every part. Nothing has to cross between parts.
Inputs may be any that keep to these rules, and one draw needn't show every extreme that they name: `routes`: A row names 2 different experts. Within the 16 rows of one device (aligned blocks) no expert is named more than 8 times, and one expert, the same in all blocks, is named exactly 8 times in every block. slots[t, k] numbers the rows of t's block that name expert routes[t, k]: within a block the slots of one expert are distinct. `lengths`: every block of 16 sequences holds one of length 128.
All inputs are finite; a program needn't handle non-finite values.
Results may differ from a plain program's by a relative error of at most 0.006.
Values may be sent and summed in bfloat16 or wider, within the bound.
No kernel may reach another device: no remote copies, remote signals or barrier semaphores. Data moves between devices by JAX's collectives and lax.ppermute only.
A program may use at most 128 MiB of HBM per device.

v0:
```python
import jax
import jax.numpy as jnp
from jax import lax
from jax.sharding import PartitionSpec as P

EXPERTS = 8


def mamba_step(
    mamba_input,
    mamba_gate,
    conv_state,
    scan_state,
    conv_weight,
    conv_bias,
    state_proj,
    step_proj,
    step_bias,
    decay_log,
    skip_gain,
):
    window = jnp.concatenate(
        [conv_state.astype(jnp.float32), mamba_input.astype(jnp.float32)[:, None, :]], axis=1
    )
    conv_act = jax.nn.silu(jnp.sum(window * conv_weight[None], axis=1) + conv_bias)
    local_mix = lax.dot_general(
        conv_act.astype(jnp.bfloat16),
        state_proj,
        (((1,), (1,)), ((), ())),
        preferred_element_type=jnp.float32,
    )
    mixing = lax.psum(local_mix, "tensor")
    low_rank = step_proj.shape[0]
    states = decay_log.shape[0]
    step_size = jax.nn.softplus(
        jnp.dot(
            mixing[:, :low_rank].astype(jnp.bfloat16), step_proj, preferred_element_type=jnp.float32
        )
        + step_bias
    )
    in_coef = mixing[:, low_rank : low_rank + states]
    out_coef = mixing[:, low_rank + states :]
    decay_rate = jnp.exp(-step_size[:, None, :] * jnp.exp(decay_log)[None])
    next_state = decay_rate * scan_state + (step_size * conv_act)[:, None, :] * in_coef[:, :, None]
    mixed_out = jnp.sum(next_state * out_coef[:, :, None], axis=1) + skip_gain * conv_act
    return (
        (mixed_out * jax.nn.silu(mamba_gate.astype(jnp.float32))).astype(jnp.bfloat16),
        next_state,
    )


def attend(queries, new_entry, past_entries, lengths):
    seq_count, head_count, head_size = queries.shape
    groups = past_entries.shape[1]
    per_group = head_count // groups
    positions = past_entries.shape[2]
    scaling = head_size ** (-0.5)
    query_rows = queries.reshape(seq_count, groups, per_group, head_size)
    scores = (
        jnp.einsum(
            "sgqd,sgld->sgql",
            query_rows,
            past_entries[..., :head_size],
            preferred_element_type=jnp.float32,
        )
        * scaling
    )
    own_score = (
        jnp.einsum(
            "sgqd,sgd->sgq",
            query_rows,
            new_entry[..., :head_size],
            preferred_element_type=jnp.float32,
        )
        * scaling
    )
    live_mask = jnp.arange(positions, dtype=jnp.int32)[None, :] < lengths[:, None]
    scores = jnp.where(live_mask[:, None, None, :], scores, -jnp.inf)
    highest = jnp.maximum(jnp.max(scores, axis=3), own_score)
    weights = jnp.exp(scores - highest[..., None])
    own_weight = jnp.exp(own_score - highest)
    denominator = jnp.sum(weights, axis=3) + own_weight
    weights_low = (weights / denominator[..., None]).astype(jnp.bfloat16)
    own_low = (own_weight / denominator).astype(jnp.bfloat16)
    mixed_out = jnp.einsum(
        "sgql,sgld->sgqd",
        weights_low,
        past_entries[..., head_size:],
        preferred_element_type=jnp.float32,
    )
    mixed_out = (
        mixed_out
        + own_low.astype(jnp.float32)[..., None]
        * new_entry[..., head_size:].astype(jnp.float32)[:, :, None, :]
    )
    return mixed_out.reshape(seq_count, head_count * head_size).astype(jnp.bfloat16)


def shards(
    mamba_input,
    mamba_gate,
    conv_state,
    scan_state,
    conv_weight,
    conv_bias,
    state_proj,
    step_proj,
    step_bias,
    decay_log,
    skip_gain,
    queries,
    new_entry,
    past_entries,
    lengths,
    expert_input,
    routes,
    slots,
    gates,
    inner_weights,
    outer_weights,
):
    peer_count = lax.axis_size("expert")
    token_count = routes.shape[0]
    capacity = max(2, 4 * token_count // EXPERTS)
    replicas = max(1, peer_count // EXPERTS)
    local_rows = inner_weights.shape[0]
    total_rows = peer_count * local_rows
    row_expert = jnp.arange(total_rows, dtype=jnp.int32) // replicas
    slot_index = jnp.arange(capacity, dtype=jnp.int32)
    matches = (row_expert[:, None, None, None] == routes[None, None, :, :]) & (
        slot_index[None, :, None, None] == slots[None, None, :, :]
    )
    send_table = jnp.any(matches, axis=3).astype(jnp.bfloat16)
    weight_table = jnp.sum(jnp.where(matches, gates[None, None, :, :], 0.0), axis=3)
    features = lax.all_gather(expert_input, "tensor", axis=1, tiled=True)
    outgoing = jnp.einsum(
        "rcb,bd->rcd", send_table, features, preferred_element_type=jnp.float32
    ).astype(jnp.bfloat16)
    outgoing = outgoing.reshape(peer_count, local_rows, capacity, features.shape[1])
    gate_rows = inner_weights[:, 0]
    up_rows = inner_weights[:, 1]
    received = lax.all_to_all(outgoing, "expert", split_axis=0, concat_axis=0, tiled=True)
    gate_val = jnp.einsum("nlcd,lfd->nlcf", received, gate_rows, preferred_element_type=jnp.float32)
    up_val = jnp.einsum("nlcd,lfd->nlcf", received, up_rows, preferred_element_type=jnp.float32)
    hidden = (jax.nn.silu(gate_val) * up_val).astype(jnp.bfloat16)
    partial_value = jnp.einsum(
        "nlcf,lfd->nlcd", hidden, outer_weights, preferred_element_type=jnp.float32
    )
    share_sum = lax.psum_scatter(partial_value, "tensor", scatter_dimension=3, tiled=True)
    returned = lax.all_to_all(share_sum, "expert", split_axis=0, concat_axis=0, tiled=True)
    returned = returned.reshape(total_rows, capacity, returned.shape[3])
    merged = jnp.einsum("rcb,rcd->bd", weight_table, returned, precision=lax.Precision.HIGHEST)
    expert_out = merged.astype(jnp.bfloat16)
    mamba_out, next_state = mamba_step(
        mamba_input,
        mamba_gate,
        conv_state,
        scan_state,
        conv_weight,
        conv_bias,
        state_proj,
        step_proj,
        step_bias,
        decay_log,
        skip_gain,
    )
    attention_out = attend(queries, new_entry, past_entries, lengths)
    return (mamba_out, next_state, attention_out, expert_out)


def solution(mesh):
    return jax.shard_map(
        shards,
        mesh=mesh,
        in_specs=(
            P(("parts", "expert"), "tensor"),
            P(("parts", "expert"), "tensor"),
            P(("parts", "expert"), None, "tensor"),
            P(("parts", "expert"), None, "tensor"),
            P(None, "tensor"),
            P("tensor"),
            P(None, "tensor"),
            P(None, "tensor"),
            P("tensor"),
            P(None, "tensor"),
            P("tensor"),
            P(("parts", "expert"), "tensor", None),
            P(("parts", "expert"), "tensor", None),
            P(("parts", "expert"), "tensor", None, None),
            P(("parts", "expert")),
            P(("parts", "expert"), "tensor"),
            P(("parts", "expert"), None),
            P(("parts", "expert"), None),
            P(("parts", "expert"), None),
            P("expert", None, "tensor", None),
            P("expert", "tensor", None),
        ),
        out_specs=(
            P(("parts", "expert"), "tensor"),
            P(("parts", "expert"), None, "tensor"),
            P(("parts", "expert"), "tensor"),
            P(("parts", "expert"), "tensor"),
        ),
        check_vma=False,
    )
```

profile of v0, /device:TPU:0, one launch (start us, length us, event | category | flops | bytes accessed | tf_op | source)
XLA Modules:
  0.0 100.1 jit_solution(2538967461487775858)
XLA Ops:
  7.2 0.7 iota_compare_fusion
  7.9 0.7 iota_compare_fusion.1
  8.6 6.4 %all_gather.3 = bf16[16,2048]{1,0:T(8,128)(2,1)S(1)} all-gather(bf16[16,512]{1,0:T(8,128)(2,1)} %param.36), channel_id=1, replica_groups=mesh['parts'=2,'expert'=4,'tensor'=4] {'tensor'}, dimensions={1}, use_global_device_ids=true | all-gather | bytes 81920 | tf_op jit(solution)/shard_map/all_gather | solution.py:135
  15.1 0.9 convolution_convert_fusion
  16.0 5.3 %all-to-all-start = ((bf16[4,2,8,2048]{3,2,1,0:T(8,128)(2,1)}), bf16[4,2,8,2048]{3,2,1,0:T(8,128)(2,1)S(1)}, u32[]{:S(2)}, u32[]{:S(2)}) async-start(bf16[4,2,8,2048]{3,2,1,0:T(8,128)(2,1)} %bitcast.6), calls=%async_computation | async-start | bytes 524288 | tf_op jit(solution)/shard_map/all_to_all | solution.py:142
  21.3 0.7 iota_compare_fusion.2
  22.0 0.7 slice_bitcast_fusion
  22.8 0.9 fusion.42
  23.7 2.0 %fusion.49 = (f32[16,2,4]{2,1,0:T(2,128)S(1)}, f32[16,2,4,128]{3,2,1,0:T(4,128)S(1)}) fusion(bf16[16,2,4,128]{3,2,1,0:T(4,128)(2,1)} %bitcast.69, bf16[16,2,128,256]{3,2,1,0:T(8,128)(2,1)} %param.34, pred[16,128]{1,0:T(8,128)(4,1)S(1)} %iota_compare_fusion.2), kind=kOutput, calls=%fused_computation.64 | convolution fusion | flops 4243328 | bytes 1149440 | tf_op jit(solution)/shard_map/sgqd,sgld->sgql/dot_general | solution.py:60
  26.0 0.9 exp.29
  26.8 1.7 %fusion.24 = bf16[16,2,4,128]{3,2,1,0:T(4,128)(2,1)S(1)} fusion(bf16[16,2,128,256]{3,2,1,0:T(8,128)(2,1)} %param.34, f32[16,2,4,128]{3,2,1,0:T(4,128)S(1)} %get-tuple-element.15, f32[16,2,128]{2,1,0:T(2,128)S(1)} %get-tuple-element.13, f32[16,2,4]{2,1,0:T(2,128)S(1)} %get-tuple-element.9, f32[16,2,4]{2,1,0:T(2,128)S(1)} %get-tuple-element.8, ...), kind=kOutput, calls=%fused_computation.18 | convolution fusion | flops 4292608 | bytes 1164800 | tf_op jit(solution)/shard_map/sgql,sgld->sgqd/dot_general | solution.py:85
  28.5 0.6 convert_element_type.48
  29.1 0.9 multiply_reduce_fusion.1
  30.7 8.4 %fusion.11 = f32[4,2,8,2048]{3,2,0,1:T(8,128)S(1)} fusion(bf16[2,2,2048,2048]{3,2,1,0:T(8,128)(2,1)} %param.40, bf16[4,2,8,2048]{3,2,1,0:T(8,128)(2,1)S(1)} %all-to-all-done), kind=kOutput, calls=%fused_computation.9 | convolution fusion | flops 536870912 | bytes 17563648 | tf_op jit(solution)/shard_map/nlcd,lfd->nlcf/dot_general | solution.py:143
  39.1 8.7 %fusion.20 = bf16[4,2,8,2048]{3,2,0,1:T(8,128)(2,1)S(1)} fusion(bf16[2,2,2048,2048]{3,2,1,0:T(8,128)(2,1)} %param.40, f32[4,2,8,2048]{3,2,0,1:T(8,128)S(1)} %fusion.11, bf16[4,2,8,2048]{3,2,1,0:T(8,128)(2,1)S(1)} %all-to-all-done), kind=kOutput, calls=%fused_computation.13 | convolution fusion | flops 537657344 | bytes 17825792 | tf_op jit(solution)/shard_map/nlcd,lfd->nlcf/dot_general | solution.py:144
  47.9 9.5 %fusion.8 = f32[4,2,8,2048]{3,2,0,1:T(8,128)} fusion(bf16[4,2,8,2048]{3,2,0,1:T(8,128)(2,1)S(1)} %fusion.20, bf16[2,2048,2048]{2,1,0:T(8,128)(2,1)} %param.41), kind=kOutput, calls=%fused_computation.8 | convolution fusion | flops 536870912 | bytes 17563648 | tf_op jit(solution)/shard_map/nlcf,lfd->nlcd/dot_general | solution.py:146
  57.7 10.7 %psum.7 = f32[16,288]{1,0:T(8,128)S(1)} all-reduce(f32[16,288]{1,0:T(8,128)S(1)} %fusion.40), channel_id=1, replica_groups=mesh['parts'=2,'expert'=4,'tensor'=4] {'tensor'}, use_global_device_ids=true, to_apply=%region_1.2 | all-reduce | flops 4608 | bytes 36864 | tf_op jit(solution)/shard_map/psum | solution.py:32
  68.8 1.5 %multiply_reduce_fusion = (f32[16,1024]{1,0:T(8,128)S(1)}, f32[16,16,1024]{2,1,0:T(8,128)}) fusion(f32[16,16]{1,0:T(8,128)S(1)} %get-tuple-element.11, f32[16,16]{1,0:T(8,128)S(1)} %get-tuple-element.10, f32[16,1024]{1,0:T(8,128)S(1)} %get-tuple-element.7, f32[16,16,1024]{2,1,0:T(8,128)S(1)} %copy-done.1, f32[16,1024]{1,0:T(8,128)S(1)} %exp.29, ...), kind=kLoop, calls=%fused_computation.23 | loop fusion | flops 1556480 | bytes 2361344 | tf_op jit(solution)/shard_map/reduce_sum | solution.py:45
  70.3 9.9 %reduce-scatter.2.cloned.1.call-done = f32[4,2,8,512]{3,2,0,1:T(8,128)} async-done(((f32[4,2,8,2048]{3,2,0,1:T(8,128)}), f32[4,2,8,512]{3,2,0,1:T(8,128)}) %reduce-scatter.2.cloned.1.call-update) | async-done | bytes 131088 | tf_op jit(solution)/shard_map/reduce_scatter | solution.py:149
  80.2 1.5 %copy.50 = f32[4,2,8,512]{3,2,1,0:T(8,128)} copy(f32[4,2,8,512]{3,2,0,1:T(8,128)} %reduce-scatter.2.cloned.1.call-done) | data formatting | bytes 262144 | tf_op jit(solution)/shard_map/reduce_scatter | solution.py:149
  81.7 4.6 %all-to-all-start.1 = ((f32[4,2,8,512]{3,2,1,0:T(8,128)}), f32[4,2,8,512]{3,2,1,0:T(8,128)S(1)}, u32[]{:S(2)}, u32[]{:S(2)}) async-start(f32[4,2,8,512]{3,2,1,0:T(8,128)} %copy.50), calls=%async_computation.2 | async-start | bytes 262144 | tf_op jit(solution)/shard_map/all_to_all | solution.py:150
  86.3 0.7 fusion.36
  87.0 5.4 %all-to-all-done.1 = f32[4,2,8,512]{3,2,1,0:T(8,128)S(1)} async-done(((f32[4,2,8,512]{3,2,1,0:T(8,128)}), f32[4,2,8,512]{3,2,1,0:T(8,128)S(1)}, u32[]{:S(2)}, u32[]{:S(2)}) %all-to-all-start.1) | async-done | bytes 131104 | tf_op jit(solution)/shard_map/all_to_all | solution.py:150
  92.4 0.8 fusion.25
  (27 shorter events, 1.5 us)
Async XLA Ops:
  7.2 50.3 %copy-start = (bf16[288,1024]{1,0:T(8,128)(2,1)S(1)}, bf16[288,1024]{1,0:T(8,128)(2,1)}, u32[]{:S(2)}) copy-start(bf16[288,1024]{1,0:T(8,128)(2,1)} %param.27) | copy-start | bytes 1769476
  16.0 14.7 %all-to-all-start = ((bf16[4,2,8,2048]{3,2,1,0:T(8,128)(2,1)}), bf16[4,2,8,2048]{3,2,1,0:T(8,128)(2,1)S(1)}, u32[]{:S(2)}, u32[]{:S(2)}) async-start(bf16[4,2,8,2048]{3,2,1,0:T(8,128)(2,1)} %bitcast.6), calls=%async_computation | async-start | bytes 524288 | tf_op jit(solution)/shard_map/all_to_all | solution.py:142
  21.3 58.9 %reduce-scatter.2.cloned.1.call-start = ((), (), s32[]{:S(2)}) async-start(), calls=%async_computation.3 | async-start | bytes 655360 | tf_op jit(solution)/shard_map/reduce_scatter | solution.py:149
  47.8 9.7 %copy-start.3 = (f32[1024]{0:T(1024)S(1)}, f32[1024]{0:T(1024)}, u32[]{:S(2)}) copy-start(f32[1024]{0:T(1024)} %param.26) | copy-start | bytes 12292
  47.8 20.6 %copy-start.5 = (f32[16,2]{0,1:T(2,128)S(1)}, f32[16,2]{0,1:T(2,128)}, u32[]{:S(2)}) copy-start(f32[16,2]{0,1:T(2,128)} %param.39) | copy-start | bytes 388
  47.8 20.7 %copy-start.6 = (bf16[256,1024]{1,0:T(8,128)(2,1)S(1)}, bf16[256,1024]{1,0:T(8,128)(2,1)}, u32[]{:S(2)}) copy-start(bf16[256,1024]{1,0:T(8,128)(2,1)} %param.28) | copy-start | bytes 1572868
  47.8 20.7 %copy-start.7 = (f32[1024]{0:T(1024)S(1)}, f32[1024]{0:T(1024)}, u32[]{:S(2)}) copy-start(f32[1024]{0:T(1024)} %param.29) | copy-start | bytes 12292
  47.9 20.9 %copy-start.1 = (f32[16,16,1024]{2,1,0:T(8,128)S(1)}, f32[16,16,1024]{2,1,0:T(8,128)}, u32[]{:S(2)}) copy-start(f32[16,16,1024]{2,1,0:T(8,128)} %param.24) | copy-start | bytes 3145732
  47.9 38.5 %copy-start.2 = (bf16[16,1024]{1,0:T(8,128)(2,1)S(1)}, bf16[16,1024]{1,0:T(8,128)(2,1)}, u32[]{:S(2)}) copy-start(bf16[16,1024]{1,0:T(8,128)(2,1)} %param.22) | copy-start | bytes 98308
  47.9 38.5 %copy-start.4 = (f32[1024]{0:T(1024)S(1)}, f32[1024]{0:T(1024)}, u32[]{:S(2)}) copy-start(f32[1024]{0:T(1024)} %param.31) | copy-start | bytes 12292
  81.7 10.7 %all-to-all-start.1 = ((f32[4,2,8,512]{3,2,1,0:T(8,128)}), f32[4,2,8,512]{3,2,1,0:T(8,128)S(1)}, u32[]{:S(2)}, u32[]{:S(2)}) async-start(f32[4,2,8,512]{3,2,1,0:T(8,128)} %copy.50), calls=%async_computation.2 | async-start | bytes 262144 | tf_op jit(solution)/shard_map/all_to_all | solution.py:150
Sparse Core Ops, SparseCore 0:
  57.6 22.5 reduce-scatter.1
where the time goes:
time: 101 us; the launch traced here: 100 us
  matrix products  33.4 us (33%)
  blocking collectives  17.1 us (17%)
  waiting for transfers between devices  16 us (16%)
  between operations  14.2 us (14%)
  starting transfers between devices  9.95 us (10%)
  other arithmetic  6.26 us (6%)
  local copies, waits for them, and re-layouts  3.17 us (3%)
    psum x1, blocking collectives, mamba_step(): mixing = lax.psum(local_mix, 'tensor')  10.7 us
    reduce_scatter x1, waiting for transfers between devices, shards(): lax.psum_scatter(partial_value, 'tensor', scatter_dimension=3, tiled=True)  9.91 us
    dot_general x1, matrix products, shards(): jnp.einsum('nlcf,lfd->nlcd', hidden, outer_weights, preferred_element_typ...  9.55 us
    dot_general x1, matrix products, shards(): jnp.einsum('nlcd,lfd->nlcf', received, up_rows, preferred_element_type=jn...  8.68 us
    dot_general x1, matrix products, shards(): jnp.einsum('nlcd,lfd->nlcf', received, gate_rows, preferred_element_type=...  8.42 us
    all_gather x1, blocking collectives, shards(): features = lax.all_gather(expert_input, 'tensor', axis=1, tiled=True)  6.44 us
    all_to_all x1, waiting for transfers between devices, shards(): lax.all_to_all(share_sum, 'expert', split_axis=0, concat_axis=0, tiled=True)  5.4 us
    all_to_all x1, starting transfers between devices, shards(): lax.all_to_all(outgoing, 'expert', split_axis=0, concat_axis=0, tiled=True)  5.34 us
  transfers between devices with their start and end apart: 3, of which 3 were waited for; matrix products, arithmetic and copies ran while one was open for 11% of the time, Pallas kernels for 0%

commit v1 on v0

--- a/solution.py
+++ b/solution.py
@@ -29,7 +29,9 @@
         (((1,), (1,)), ((), ())),
         preferred_element_type=jnp.float32,
     )
-    mixing = lax.psum(local_mix, "tensor")
+    mixing = local_mix
+    for hop in (1, 2):
+        mixing = mixing + lax.ppermute(mixing, "tensor", [(dev, dev ^ hop) for dev in range(4)])
     low_rank = step_proj.shape[0]
     states = decay_log.shape[0]
     step_size = jax.nn.softplus(

time: 101 us -> 101 us (level)
  blocking collectives: 17.1 us -> 6.37 us
  waiting for transfers between devices: 16 us -> 25.4 us
  starting transfers between devices: 9.95 us -> 11.6 us
    psum x1 -> x0, blocking collectives: 10.7 us -> none  [mamba_step(): mixing = lax.psum(local_mix, 'tensor')]
    all_to_all x1, waiting for transfers between devices: 0.62 us -> 4.73 us  [shards(): lax.all_to_all(outgoing, 'expert', split_axis=0, concat_axis=0, tiled=True)]
    reduce_scatter x1, waiting for transfers between devices: 9.91 us -> 13.6 us  [shards(): lax.psum_scatter(partial_value, 'tensor', scatter_dimension=3, tiled=True)]
    ppermute x0 -> x2, starting transfers between devices: none -> 2.07 us  [mamba_step(): lax.ppermute(mixing, 'tensor', [(dev, dev ^ hop) for dev in range(4)])]
    ppermute x0 -> x2, waiting for transfers between devices: none -> 1.65 us  [mamba_step(): lax.ppermute(mixing, 'tensor', [(dev, dev ^ hop) for dev in range(4)])]
  transfers between devices with their start and end apart: 3 -> 5, of which waited for: 3 -> 4; matrix products, arithmetic and copies ran while one was open for 11% -> 38% of each run, Pallas kernels for 0% -> 0%
where the time goes in v1:
time: 101 us; the launch traced here: 100 us
  matrix products  34.1 us (34%)
  waiting for transfers between devices  25.4 us (25%)
  between operations  14.2 us (14%)
  starting transfers between devices  11.6 us (11%)
  blocking collectives  6.37 us (6%)
  other arithmetic  6.26 us (6%)
  local copies, waits for them, and re-layouts  2.48 us (2%)
    reduce_scatter x1, waiting for transfers between devices, shards(): lax.psum_scatter(partial_value, 'tensor', scatter_dimension=3, tiled=True)  13.6 us
    dot_general x1, matrix products, shards(): jnp.einsum('nlcf,lfd->nlcd', hidden, outer_weights, preferred_element_typ...  9.54 us
    dot_general x1, matrix products, shards(): jnp.einsum('nlcd,lfd->nlcf', received, up_rows, preferred_element_type=jn...  8.67 us
    dot_general x1, matrix products, shards(): jnp.einsum('nlcd,lfd->nlcf', received, gate_rows, preferred_element_type=...  8.42 us
    all_gather x1, blocking collectives, shards(): features = lax.all_gather(expert_input, 'tensor', axis=1, tiled=True)  6.37 us
    all_to_all x1, waiting for transfers between devices, shards(): lax.all_to_all(share_sum, 'expert', split_axis=0, concat_axis=0, tiled=True)  5.4 us
    all_to_all x1, starting transfers between devices, shards(): lax.all_to_all(outgoing, 'expert', split_axis=0, concat_axis=0, tiled=True)  4.92 us
    all_to_all x1, waiting for transfers between devices, shards(): lax.all_to_all(outgoing, 'expert', split_axis=0, concat_axis=0, tiled=True)  4.73 us
  transfers between devices with their start and end apart: 5, of which 4 were waited for; matrix products, arithmetic and copies ran while one was open for 38% of the time, Pallas kernels for 0%

profile of v1, /device:TPU:0, one launch (start us, length us, event | category | flops | bytes accessed | tf_op | source)
XLA Modules:
  0.0 100.3 jit_solution(13140190848744721310)
XLA Ops:
  7.2 1.0 multiply_reduce_fusion.1
  8.3 0.9 fusion.40
  9.8 0.7 iota_compare_fusion
  10.5 0.7 iota_compare_fusion.1
  11.1 6.4 %all_gather.3 = bf16[16,2048]{1,0:T(8,128)(2,1)S(1)} all-gather(bf16[16,512]{1,0:T(8,128)(2,1)} %param.36), channel_id=1, replica_groups=mesh['parts'=2,'expert'=4,'tensor'=4] {'tensor'}, dimensions={1}, use_global_device_ids=true | all-gather | bytes 81920 | tf_op jit(solution)/shard_map/all_gather | solution.py:137
  17.5 0.9 convolution_convert_fusion
  18.4 4.9 %all-to-all-start = ((bf16[4,2,8,2048]{3,2,1,0:T(8,128)(2,1)}), bf16[4,2,8,2048]{3,2,1,0:T(8,128)(2,1)S(1)}, u32[]{:S(2)}, u32[]{:S(2)}) async-start(bf16[4,2,8,2048]{3,2,1,0:T(8,128)(2,1)} %bitcast.6), calls=%async_computation | async-start | bytes 524288 | tf_op jit(solution)/shard_map/all_to_all | solution.py:144
  23.4 0.7 iota_compare_fusion.2
  24.1 0.7 slice_bitcast_fusion
  24.8 0.9 fusion.42
  25.7 2.0 %fusion.49 = (f32[16,2,4]{2,1,0:T(2,128)S(1)}, f32[16,2,4,128]{3,2,1,0:T(4,128)S(1)}) fusion(bf16[16,2,4,128]{3,2,1,0:T(4,128)(2,1)} %bitcast.69, bf16[16,2,128,256]{3,2,1,0:T(8,128)(2,1)} %param.34, pred[16,128]{1,0:T(8,128)(4,1)S(1)} %iota_compare_fusion.2), kind=kOutput, calls=%fused_computation.64 | convolution fusion | flops 4243328 | bytes 1149440 | tf_op jit(solution)/shard_map/sgqd,sgld->sgql/dot_general | solution.py:62
  28.0 4.7 %all-to-all-done = bf16[4,2,8,2048]{3,2,1,0:T(8,128)(2,1)S(1)} async-done(((bf16[4,2,8,2048]{3,2,1,0:T(8,128)(2,1)}), bf16[4,2,8,2048]{3,2,1,0:T(8,128)(2,1)S(1)}, u32[]{:S(2)}, u32[]{:S(2)}) %all-to-all-start) | async-done | bytes 262176 | tf_op jit(solution)/shard_map/all_to_all | solution.py:144
  32.7 8.4 %fusion.11 = f32[4,2,8,2048]{3,2,0,1:T(8,128)S(1)} fusion(bf16[2,2,2048,2048]{3,2,1,0:T(8,128)(2,1)} %param.40, bf16[4,2,8,2048]{3,2,1,0:T(8,128)(2,1)S(1)} %all-to-all-done), kind=kOutput, calls=%fused_computation.9 | convolution fusion | flops 536870912 | bytes 17563648 | tf_op jit(solution)/shard_map/nlcd,lfd->nlcf/dot_general | solution.py:145
  41.2 8.7 %fusion.20 = bf16[4,2,8,2048]{3,2,0,1:T(8,128)(2,1)S(1)} fusion(bf16[2,2,2048,2048]{3,2,1,0:T(8,128)(2,1)} %param.40, f32[4,2,8,2048]{3,2,0,1:T(8,128)S(1)} %fusion.11, bf16[4,2,8,2048]{3,2,1,0:T(8,128)(2,1)S(1)} %all-to-all-done), kind=kOutput, calls=%fused_computation.13 | convolution fusion | flops 537657344 | bytes 17825792 | tf_op jit(solution)/shard_map/nlcd,lfd->nlcf/dot_general | solution.py:146
  49.9 9.5 %fusion.8 = f32[4,2,8,2048]{3,2,0,1:T(8,128)} fusion(bf16[4,2,8,2048]{3,2,0,1:T(8,128)(2,1)S(1)} %fusion.20, bf16[2,2048,2048]{2,1,0:T(8,128)(2,1)} %param.41), kind=kOutput, calls=%fused_computation.8 | convolution fusion | flops 536870912 | bytes 17563648 | tf_op jit(solution)/shard_map/nlcf,lfd->nlcd/dot_general | solution.py:148
  59.5 1.7 %fusion.24 = bf16[16,2,4,128]{3,2,1,0:T(4,128)(2,1)S(1)} fusion(bf16[16,2,128,256]{3,2,1,0:T(8,128)(2,1)} %param.34, f32[16,2,4,128]{3,2,1,0:T(4,128)S(1)} %get-tuple-element.15, f32[16,2,128]{2,1,0:T(2,128)S(1)} %get-tuple-element.13, f32[16,2,4]{2,1,0:T(2,128)S(1)} %get-tuple-element.9, f32[16,2,4]{2,1,0:T(2,128)S(1)} %get-tuple-element.8, ...), kind=kOutput, calls=%fused_computation.18 | convolution fusion | flops 4292608 | bytes 1164800 | tf_op jit(solution)/shard_map/sgql,sgld->sgqd/dot_general | solution.py:87
  61.2 1.6 %collective-permute-start.1 = (f32[16,288]{1,0:T(8,128)S(1)}, f32[16,288]{1,0:T(8,128)S(1)}, u32[]{:S(2)}, u32[]{:S(2)}) collective-permute-start(f32[16,288]{1,0:T(8,128)S(1)} %add.56), channel_id=1, source_target_pairs={{0,2},{1,3},{2,0},{3,1},{4,6},{5,7},{6,4},{7,5},{8,10},{9,11},{10,... | collective-permute-start | bytes 55304 | tf_op jit(solution)/shard_map/ppermute | solution.py:34
  63.4 1.6 %collective-permute-done.1 = f32[16,288]{1,0:T(8,128)S(1)} collective-permute-done((f32[16,288]{1,0:T(8,128)S(1)}, f32[16,288]{1,0:T(8,128)S(1)}, u32[]{:S(2)}, u32[]{:S(2)}) %collective-permute-start.1) | collective-permute-done | bytes 18464 | tf_op jit(solution)/shard_map/ppermute | solution.py:34
  65.4 1.5 %multiply_reduce_fusion = (f32[16,1024]{1,0:T(8,128)S(1)}, f32[16,16,1024]{2,1,0:T(8,128)}) fusion(f32[16,16]{1,0:T(8,128)S(1)} %get-tuple-element.11, f32[16,16]{1,0:T(8,128)S(1)} %get-tuple-element.10, f32[16,1024]{1,0:T(8,128)S(1)} %get-tuple-element.7, f32[16,16,1024]{2,1,0:T(8,128)S(1)} %copy-done.1, f32[16,1024]{1,0:T(8,128)S(1)} %exp.29, ...), kind=kLoop, calls=%fused_computation.23 | loop fusion | flops 1556480 | bytes 2361344 | tf_op jit(solution)/shard_map/reduce_sum | solution.py:47
  66.9 13.6 %reduce-scatter.2.cloned.1.call-done = f32[4,2,8,512]{3,2,0,1:T(8,128)} async-done(((f32[4,2,8,2048]{3,2,0,1:T(8,128)}), f32[4,2,8,512]{3,2,0,1:T(8,128)}) %reduce-scatter.2.cloned.1.call-update) | async-done | bytes 131088 | tf_op jit(solution)/shard_map/reduce_scatter | solution.py:151
  80.4 1.6 %copy.50 = f32[4,2,8,512]{3,2,1,0:T(8,128)} copy(f32[4,2,8,512]{3,2,0,1:T(8,128)} %reduce-scatter.2.cloned.1.call-done) | data formatting | bytes 262144 | tf_op jit(solution)/shard_map/reduce_scatter | solution.py:151
  82.0 4.6 %all-to-all-start.1 = ((f32[4,2,8,512]{3,2,1,0:T(8,128)}), f32[4,2,8,512]{3,2,1,0:T(8,128)S(1)}, u32[]{:S(2)}, u32[]{:S(2)}) async-start(f32[4,2,8,512]{3,2,1,0:T(8,128)} %copy.50), calls=%async_computation.2 | async-start | bytes 262144 | tf_op jit(solution)/shard_map/all_to_all | solution.py:152
  87.3 5.4 %all-to-all-done.1 = f32[4,2,8,512]{3,2,1,0:T(8,128)S(1)} async-done(((f32[4,2,8,512]{3,2,1,0:T(8,128)}), f32[4,2,8,512]{3,2,1,0:T(8,128)S(1)}, u32[]{:S(2)}, u32[]{:S(2)}) %all-to-all-start.1) | async-done | bytes 131104 | tf_op jit(solution)/shard_map/all_to_all | solution.py:152
  92.7 0.8 fusion.25
  (34 shorter events, 2.7 us)
Async XLA Ops:
  7.2 1.1 %copy-start = (bf16[288,1024]{1,0:T(8,128)(2,1)S(1)}, bf16[288,1024]{1,0:T(8,128)(2,1)}, u32[]{:S(2)}) copy-start(bf16[288,1024]{1,0:T(8,128)(2,1)} %param.27) | copy-start | bytes 1769476
  9.3 51.9 %collective-permute-start = (f32[16,288]{1,0:T(8,128)S(1)}, f32[16,288]{1,0:T(8,128)S(1)}, u32[]{:S(2)}, u32[]{:S(2)}) collective-permute-start(f32[16,288]{1,0:T(8,128)S(1)} %fusion.40), channel_id=1, source_target_pairs={{0,1},{1,0},{2,3},{3,2},{4,5},{5,4},{6,7},{7,6},{8,9},{9,8},{10,11... | collective-permute-start | bytes 55304 | tf_op jit(solution)/shard_map/ppermute | solution.py:34
  18.4 14.3 %all-to-all-start = ((bf16[4,2,8,2048]{3,2,1,0:T(8,128)(2,1)}), bf16[4,2,8,2048]{3,2,1,0:T(8,128)(2,1)S(1)}, u32[]{:S(2)}, u32[]{:S(2)}) async-start(bf16[4,2,8,2048]{3,2,1,0:T(8,128)(2,1)} %bitcast.6), calls=%async_computation | async-start | bytes 524288 | tf_op jit(solution)/shard_map/all_to_all | solution.py:144
  23.4 57.1 %reduce-scatter.2.cloned.1.call-start = ((), (), s32[]{:S(2)}) async-start(), calls=%async_computation.3 | async-start | bytes 655360 | tf_op jit(solution)/shard_map/reduce_scatter | solution.py:151
  49.8 12.9 %copy-start.6 = (f32[16,2]{0,1:T(2,128)S(1)}, f32[16,2]{0,1:T(2,128)}, u32[]{:S(2)}) copy-start(f32[16,2]{0,1:T(2,128)} %param.39) | copy-start | bytes 388
  49.9 12.9 %copy-start.2 = (f32[16,1024]{1,0:T(8,128)S(1)}, f32[16,1024]{1,0:T(8,128)}, u32[]{:S(2)}) copy-start(f32[16,1024]{1,0:T(8,128)} %param.30) | copy-start | bytes 196612
  49.9 15.3 %copy-start.4 = (f32[1024]{0:T(1024)S(1)}, f32[1024]{0:T(1024)}, u32[]{:S(2)}) copy-start(f32[1024]{0:T(1024)} %param.26) | copy-start | bytes 12292
  49.9 15.3 %copy-start.7 = (bf16[256,1024]{1,0:T(8,128)(2,1)S(1)}, bf16[256,1024]{1,0:T(8,128)(2,1)}, u32[]{:S(2)}) copy-start(bf16[256,1024]{1,0:T(8,128)(2,1)} %param.28) | copy-start | bytes 1572868
  49.9 15.3 %copy-start.8 = (f32[1024]{0:T(1024)S(1)}, f32[1024]{0:T(1024)}, u32[]{:S(2)}) copy-start(f32[1024]{0:T(1024)} %param.29) | copy-start | bytes 12292
  49.9 15.5 %copy-start.1 = (f32[16,16,1024]{2,1,0:T(8,128)S(1)}, f32[16,16,1024]{2,1,0:T(8,128)}, u32[]{:S(2)}) copy-start(f32[16,16,1024]{2,1,0:T(8,128)} %param.24) | copy-start | bytes 3145732
  49.9 36.7 %copy-start.3 = (bf16[16,1024]{1,0:T(8,128)(2,1)S(1)}, bf16[16,1024]{1,0:T(8,128)(2,1)}, u32[]{:S(2)}) copy-start(bf16[16,1024]{1,0:T(8,128)(2,1)} %param.22) | copy-start | bytes 98308
  49.9 36.7 %copy-start.5 = (f32[1024]{0:T(1024)S(1)}, f32[1024]{0:T(1024)}, u32[]{:S(2)}) copy-start(f32[1024]{0:T(1024)} %param.31) | copy-start | bytes 12292
  61.2 3.9 %collective-permute-start.1 = (f32[16,288]{1,0:T(8,128)S(1)}, f32[16,288]{1,0:T(8,128)S(1)}, u32[]{:S(2)}, u32[]{:S(2)}) collective-permute-start(f32[16,288]{1,0:T(8,128)S(1)} %add.56), channel_id=1, source_target_pairs={{0,2},{1,3},{2,0},{3,1},{4,6},{5,7},{6,4},{7,5},{8,10},{9,11},{10,... | collective-permute-start | bytes 55304 | tf_op jit(solution)/shard_map/ppermute | solution.py:34
  82.0 10.6 %all-to-all-start.1 = ((f32[4,2,8,512]{3,2,1,0:T(8,128)}), f32[4,2,8,512]{3,2,1,0:T(8,128)S(1)}, u32[]{:S(2)}, u32[]{:S(2)}) async-start(f32[4,2,8,512]{3,2,1,0:T(8,128)} %copy.50), calls=%async_computation.2 | async-start | bytes 262144 | tf_op jit(solution)/shard_map/all_to_all | solution.py:152
Sparse Core Ops, SparseCore 0:
  59.6 20.7 reduce-scatter.1
